TPU v7x, 16 devices: a whole 2x2x2 slice. The times are simulated.
16 devices in a mesh: tp: 2 (over z), fsdp: 8 (over y, x, core).
Axes of the slice: x: 2, y: 2, z: 2, core: 2. Of those that a mesh axis runs over, the one named last changes fastest.
Arguments:
- emb_table: float32 [2048, 1152], P('tp', 'fsdp')
- tok_ids: int32 [32, 4096], P('fsdp')
- lab_ids: int32 [32, 4096], P('fsdp')
- h_last: bfloat16 [32, 4096, 1152], P('fsdp')
- g_embed: bfloat16 [32, 4096, 1152], P('fsdp')
- norm_w: float32 [1152], P('fsdp')
Outputs:
- output 1: bfloat16 [32, 4096, 1152], P('fsdp')
- output 2: float32 [], replicated
- output 3: bfloat16 [32, 4096, 1152], P('fsdp')
- output 4: float32 [1152], P('fsdp')
- output 5: float32 [2048, 1152], P('tp', 'fsdp')
All inputs are finite; a program needn't handle non-finite values.
Results may differ from a plain program's by a relative error of at most 0.001.
Values are sent between devices in bfloat16 or wider.
A program may use at most 1 GiB of HBM per device.

v0:
```python
import math
import jax
import jax.numpy as jnp
from jax import lax
from jax.sharding import PartitionSpec as P

SOFT_CAP = 30.0
NORM_EPS = 1e-6


def solution(mesh):
    fsdp_size = mesh.shape["fsdp"]

    def device_step(emb_shard, tok_ids, lab_ids, h_last, g_embed, norm_w):
        vocab_rows = emb_shard.shape[0]
        batch_loc, seq_len, width = h_last.shape
        tok_count = batch_loc * seq_len
        total_tokens = tok_count * fsdp_size
        row_start = lax.axis_index("tp") * vocab_rows
        vocab_iota = jnp.arange(vocab_rows, dtype=jnp.int32)
        emb_scale = jnp.asarray(math.sqrt(width), jnp.bfloat16).astype(jnp.float32)
        shard_bf = emb_shard.astype(jnp.bfloat16)

        table_look = lax.all_gather(shard_bf, "fsdp", axis=1, tiled=True)
        tok_local = tok_ids.reshape(tok_count) - row_start
        in_block = (tok_local >= 0) & (tok_local < vocab_rows)
        row_vals = jnp.take(table_look, jnp.clip(tok_local, 0, vocab_rows - 1), axis=0)
        row_vals = lax.psum(jnp.where(in_block[:, None], row_vals, jnp.zeros_like(row_vals)), "tp")
        x_emb = (row_vals.astype(jnp.float32) * emb_scale).astype(jnp.bfloat16)

        norm_gain = 1.0 + lax.all_gather(norm_w, "fsdp", axis=0, tiled=True)
        h_wide = h_last.reshape(tok_count, width).astype(jnp.float32)
        inv_rms = lax.rsqrt(jnp.mean(h_wide * h_wide, axis=1, keepdims=True) + NORM_EPS)
        h_norm = h_wide * inv_rms
        x_norm = (h_norm * norm_gain).astype(jnp.bfloat16)

        table_head = lax.all_gather(shard_bf, "fsdp", axis=1, tiled=True)
        logits = jnp.einsum("td,vd->tv", x_norm, table_head, preferred_element_type=jnp.float32)
        tanh_z = jnp.tanh(logits / SOFT_CAP)
        capped = SOFT_CAP * tanh_z
        exp_shift = jnp.exp(capped - SOFT_CAP)
        lab_hit = (lab_ids.reshape(tok_count) - row_start)[:, None] == vocab_iota[None, :]
        tok_stats = jnp.stack([jnp.sum(exp_shift, axis=1), jnp.sum(jnp.where(lab_hit, capped, 0.0), axis=1)])
        tok_stats = lax.psum(tok_stats, "tp")
        sum_exp = tok_stats[0]
        log_norm = jnp.log(sum_exp) + SOFT_CAP
        loss_val = lax.psum(jnp.sum(log_norm - tok_stats[1]), "fsdp") / total_tokens

        soft_prob = exp_shift / sum_exp[:, None]
        d_logits = ((soft_prob - lab_hit.astype(jnp.float32)) * (1.0 - tanh_z * tanh_z) / total_tokens).astype(jnp.bfloat16)
        d_xnorm = lax.psum(jnp.dot(d_logits, table_head, preferred_element_type=jnp.float32), "tp")
        g_dir = d_xnorm * norm_gain
        d_hidden = (inv_rms * (g_dir - h_norm * jnp.mean(g_dir * h_norm, axis=1, keepdims=True))).astype(jnp.bfloat16)
        d_norm_w = lax.psum_scatter(jnp.sum(d_xnorm * h_norm, axis=0), "fsdp", scatter_dimension=0, tiled=True)

        head_part = jnp.einsum("tv,td->vd", d_logits, x_norm, preferred_element_type=jnp.float32)
        d_head = lax.psum_scatter(head_part, "fsdp", scatter_dimension=1, tiled=True)
        tok_hit = (tok_local[:, None] == vocab_iota[None, :]).astype(jnp.bfloat16)
        look_part = jnp.einsum("tv,td->vd", tok_hit, g_embed.reshape(tok_count, width), preferred_element_type=jnp.float32)
        d_look = lax.psum_scatter(look_part, "fsdp", scatter_dimension=1, tiled=True)
        d_table = d_head + emb_scale * d_look
        return (x_emb.reshape(batch_loc, seq_len, width), loss_val, d_hidden.reshape(batch_loc, seq_len, width), d_norm_w, d_table)

    spec_tok = P("fsdp", None)
    spec_act = P("fsdp", None, None)
    return jax.shard_map(device_step, mesh=mesh, in_specs=(P("tp", "fsdp"), spec_tok, spec_tok, spec_act, spec_act, P("fsdp")), out_specs=(spec_act, P(), spec_act, P("fsdp"), P("tp", "fsdp")), check_vma=False)
```

profile of v0, /device:TPU:0, one launch (start us, length us, event | category | flops | bytes accessed | tf_op | source)
XLA Modules:
  0.0 2985.6 jit_solution(5073411721018362296)
XLA Ops:
  7.2 1.8 convert_element_type.31
  9.1 1.3 fusion.4
  11.1 0.9 dynamic-update-slice
  12.0 15.7 all-reduce
  27.8 22.7 multiply_reduce_fusion.2
  50.5 25.7 multiply_convert_fusion.1
  76.2 0.7 subtract_bitcast_fusion.1
  76.9 0.6 copy-done.3
  77.5 11.6 iota_compare_fusion.5
  89.1 69.3 %fusion.1 = (f32[16384]{0:T(1024)S(1)}, f32[16384]{0:T(1024)S(1)}, f32[16384,1024]{0,1:T(8,128)}) fusion(s32[16384]{0:T(1024)S(1)} %bitcast.52, bf16[16384,1152]{1,0:T(8,128)(2,1)} %multiply_convert_fusion.1, bf16[1024,1152]{0,1:T(8,128)(2,1)} %all-gather.2.cloned.1.call-done), kind=kOutput, calls=%fused_computation.15 | convolution fusion | flops 38772113408 | bytes 107413504 | tf_op jit(solution)/shard_map/td,vd->tv/dot_general | solution.py:38
  158.4 0.8 pad_maximum_fusion
  159.2 0.2 reduce-scatter.5.cloned.1.call-start
  159.5 46.2 %fusion = f32[1024,1152]{0,1:T(8,128)} fusion(bf16[16384,1152]{1,0:T(8,128)(2,1)} %bitcast.59, pred[16384,1024]{1,0:T(32,128)(4,1)} %iota_compare_fusion.5), kind=kOutput, calls=%fused_computation.14 | convolution fusion | flops 38654705664 | bytes 59244544 | tf_op jit(solution)/shard_map/tv,td->vd/dot_general | solution.py:59
  205.7 0.6 compare_and_fusion.1
  206.5 3.0 copy.12
  209.5 70.5 %gather_fusion = bf16[16384,1152]{1,0:T(8,128)(2,1)} fusion(bf16[1024,1152]{1,0:T(8,128)(2,1)S(1)} %copy.12, s32[16384]{0:T(1024)S(1)} %broadcast_clamp_fusion), kind=kCustom, calls=%fused_computation | custom fusion | bytes 75563008 | tf_op jit(solution)/shard_map/jit(_take)/gather | solution.py:27
  280.1 1.7 fusion.3
  281.8 37.6 %multiply_convert_fusion.3 = bf16[16384,1024]{0,1:T(8,128)(2,1)} fusion(f32[16384,1024]{0,1:T(8,128)} %get-tuple-element.19, f32[16384]{0:T(1024)S(1)} %bitcast.50, s32[16384]{0:T(1024)S(1)} %bitcast.53), kind=kLoop, calls=%fused_computation.9 | loop fusion | flops 201326592 | bytes 100794368 | tf_op jit(solution)/shard_map/convert_element_type | solution.py:50
  319.4 47.0 %fusion.6 = f32[1024,1152]{0,1:T(8,128)} fusion(bf16[16384,1024]{0,1:T(8,128)(2,1)} %multiply_convert_fusion.3, bf16[16384,1152]{1,0:T(8,128)(2,1)} %multiply_convert_fusion.1), kind=kOutput, calls=%fused_computation.35 | convolution fusion | flops 38654705664 | bytes 76021760 | tf_op jit(solution)/shard_map/tv,td->vd/dot_general | solution.py:56
  366.5 25.9 select_select_fusion
  392.4 0.3 all-reduce.11.cloned.1.call-start
  392.6 52.3 %fusion.5 = f32[16384,1152]{1,0:T(8,128)} fusion(bf16[16384,1024]{0,1:T(8,128)(2,1)} %multiply_convert_fusion.3, bf16[1024,1152]{0,1:T(8,128)(2,1)S(1)} %copy-done), kind=kOutput, calls=%fused_computation.34 | convolution fusion | flops 38654705664 | bytes 111411200 | tf_op jit(solution)/shard_map/dot_general | solution.py:51
  445.6 0.1 copy-done.6
  445.8 0.6 subtract_reduce_fusion
  446.4 2.1 multiply_add_fusion
  448.6 791.5 %all-reduce.7.cloned.1.call-done = bf16[16384,1152]{1,0:T(8,128)(2,1)} async-done(((bf16[16384,1152]{1,0:T(8,128)(2,1)}), bf16[16384,1152]{1,0:T(8,128)(2,1)}) %all-reduce.7.cloned.1.call-update) | async-done | bytes 37748752 | tf_op jit(solution)/shard_map/psum | solution.py:28
  1240.0 26.0 multiply_convert_fusion.2
  1266.0 1612.9 %all-reduce.11.cloned.1.call-done = f32[16384,1152]{1,0:T(8,128)} async-done(((f32[16384,1152]{1,0:T(8,128)}), f32[16384,1152]{1,0:T(8,128)}) %all-reduce.11.cloned.1.call-update) | async-done | bytes 75497488 | tf_op jit(solution)/shard_map/psum | solution.py:51
  2878.9 34.8 %multiply_reduce_fusion = (f32[1152]{0:T(1024)S(1)}, f32[16384]{0:T(1024)S(1)}) fusion(f32[16384,1152]{1,0:T(8,128)} %all-reduce.11.cloned.1.call-done, bf16[4,4096,1152]{2,1,0:T(8,128)(2,1)} %param.9, f32[16384]{0:T(1024)S(1)} %bitcast.46, f32[1152]{0:T(1024)S(1)} %copy-done.12), kind=kLoop, calls=%fused_computation.2 | loop fusion | flops 132103040 | bytes 113386496 | tf_op jit(solution)/shard_map/reduce_sum | solution.py:54
  2913.7 14.7 all-reduce.2
  2929.1 0.6 dynamic-slice.2
  2929.7 47.9 %multiply_convert_fusion = bf16[16384,1152]{1,0:T(8,128)(2,1)} fusion(f32[16384,1152]{1,0:T(8,128)} %all-reduce.11.cloned.1.call-done, bf16[4,4096,1152]{2,1,0:T(8,128)(2,1)} %param.9, f32[16384]{0:T(1024)S(1)} %broadcast_multiply_fusion, f32[1152]{0:T(1024)S(1)} %copy-done.12, f32[16384]{0:T(1024)S(1)} %bitcast.47), kind=kLoop, calls=%fused_computation.3 | loop fusion | flops 132120576 | bytes 151130624 | tf_op jit(solution)/shard_map/convert_element_type | solution.py:53
  (56 shorter events, 0.6 us)
Async XLA Ops:
  7.2 69.0 %copy-start.14 = (s32[4,4096]{1,0:T(4,128)S(1)}, s32[4,4096]{1,0:T(4,128)}, u32[]{:S(2)}) copy-start(s32[4,4096]{1,0:T(4,128)} %param.8) | copy-start | bytes 196612
  7.2 69.0 %copy-start.13 = (s32[4,4096]{1,0:T(4,128)S(1)}, s32[4,4096]{1,0:T(4,128)}, u32[]{:S(2)}) copy-start(s32[4,4096]{1,0:T(4,128)} %param.7) | copy-start | bytes 196612
  7.2 82.0 %all-gather.2.cloned.1.call-start = ((), (), s32[]{:S(2)}) async-start(), calls=%async_computation.2 | async-start | bytes 2654208 | tf_op jit(solution)/shard_map/all_gather | solution.py:24
  9.1 271.0 %all-reduce.9.cloned.1.call-start = ((), (), s32[]{:S(2)}) async-start(), calls=%async_computation.4 | async-start | bytes 262144 | tf_op jit(solution)/shard_map/psum | solution.py:44
  27.8 49.1 %copy-start.11 = (f32[1152]{0:T(1024)}, f32[1152]{0:T(1024)S(1)}, u32[]{:S(2)}) copy-start(f32[1152]{0:T(1024)S(1)} %broadcast_add_fusion) | copy-start | bytes 13828
  50.5 107.9 %copy-start.1 = (f32[1,32,4,128]{3,1,2,0:T(8,128)}, f32[1,32,4,128]{3,1,2,0:T(8,128)S(1)}, u32[]{:S(2)}) copy-start(f32[1,32,4,128]{3,1,2,0:T(8,128)S(1)} %copy.15) | copy-start | bytes 196612
  76.9 0.6 copy-start.3
  76.9 81.5 %copy-start.7 = (s32[1,32,4,128]{3,1,2,0:T(8,128)}, s32[1,32,4,128]{3,1,2,0:T(8,128)S(1)}, u32[]{:S(2)}) copy-start(s32[1,32,4,128]{3,1,2,0:T(8,128)S(1)} %copy.16) | copy-start | bytes 196612
  159.2 287.2 %reduce-scatter.5.cloned.1.call-start = ((), (), s32[]{:S(2)}) async-start(), calls=%async_computation.7 | async-start | bytes 5308416 | tf_op jit(solution)/shard_map/reduce_scatter | solution.py:60
  159.4 46.3 %copy-start.4 = (s32[1,32,4,128]{3,1,2,0:T(8,128)S(1)}, s32[1,32,4,128]{3,1,2,0:T(8,128)}, u32[]{:S(2)}) copy-start(s32[1,32,4,128]{3,1,2,0:T(8,128)} %copy-done.3) | copy-start | bytes 196612
  159.4 46.9 %copy-start.9 = (s32[1,1,4,4096]{3,2,1,0:T(4,128)S(1)}, s32[1,1,4,4096]{3,2,1,0:T(4,128)}, u32[]{:S(2)}) copy-start(s32[1,1,4,4096]{3,2,1,0:T(4,128)} %get-tuple-element.16) | copy-start | bytes 196612
  205.6 240.8 %reduce-scatter.3.cloned.1.call-start = ((), (), s32[]{:S(2)}) async-start(), calls=%async_computation.6 | async-start | bytes 5308416 | tf_op jit(solution)/shard_map/reduce_scatter | solution.py:57
  209.5 72.3 %copy-start.8 = (s32[1,32,4,128]{3,1,2,0:T(8,128)S(1)}, s32[1,32,4,128]{3,1,2,0:T(8,128)}, u32[]{:S(2)}) copy-start(s32[1,32,4,128]{3,1,2,0:T(8,128)} %copy-done.7) | copy-start | bytes 196612
  281.8 37.6 %copy-start.5 = (f32[1,16384]{1,0:T(1,128)}, f32[1,16384]{1,0:T(1,128)S(1)}, u32[]{:S(2)}) copy-start(f32[1,16384]{1,0:T(1,128)S(1)} %get-tuple-element.11) | copy-start | bytes 196612
  319.4 47.1 %copy-start.15 = (pred[16384]{0:T(1024)(128)(4,1)S(1)}, pred[16384]{0:T(1024)(128)(4,1)}, u32[]{:S(2)}) copy-start(pred[16384]{0:T(1024)(128)(4,1)} %get-tuple-element.13) | copy-start | bytes 49156
  319.4 47.1 %copy-start.16 = (pred[16384]{0:T(1024)(128)(4,1)S(1)}, pred[16384]{0:T(1024)(128)(4,1)}, u32[]{:S(2)}) copy-start(pred[16384]{0:T(1024)(128)(4,1)} %get-tuple-element.14) | copy-start | bytes 49156
  366.4 26.3 copy-start
  366.4 873.6 %all-reduce.7.cloned.1.call-start = ((), (), s32[]{:S(2)}) async-start(), calls=%async_computation.3 | async-start | bytes 75497472 | tf_op jit(solution)/shard_map/psum | solution.py:28
  392.4 2486.6 %all-reduce.11.cloned.1.call-start = ((), (), s32[]{:S(2)}) async-start(), calls=%async_computation.5 | async-start | bytes 150994944 | tf_op jit(solution)/shard_map/psum | solution.py:51
  444.9 0.8 copy-start.6
  444.9 0.9 copy-start.10
  444.9 2434.0 %copy-start.2 = (f32[1,32,4,128]{3,1,2,0:T(8,128)S(1)}, f32[1,32,4,128]{3,1,2,0:T(8,128)}, u32[]{:S(2)}) copy-start(f32[1,32,4,128]{3,1,2,0:T(8,128)} %copy-done.1) | copy-start | bytes 196612
  444.9 2434.0 %copy-start.12 = (f32[1152]{0:T(1024)S(1)}, f32[1152]{0:T(1024)}, u32[]{:S(2)}) copy-start(f32[1152]{0:T(1024)} %copy-done.11) | copy-start | bytes 13828
Sparse Core Ops, SparseCore 0:
  10.4 27.8 all-gather.1
  159.3 16.8 all-reduce.8
  205.8 47.0 reduce-scatter.4
  366.5 46.9 reduce-scatter.2
  416.4 823.5 all-reduce.6
  1242.4 1636.5 all-reduce.10
where the time goes:
time: 2990 us
  waiting for transfers between devices  2400 us (80%)
  other arithmetic  239 us (8%)
  matrix products  215 us (7%)
  local copies, waits for them, and re-layouts  79 us (3%)
  blocking collectives  30.5 us (1%)
    psum x1, waiting for transfers between devices, device_step(): lax.psum(jnp.dot(d_logits, table_head, preferred_element_type=jnp.float32...  1610 us
    psum x1, waiting for transfers between devices, device_step(): lax.psum(jnp.where(in_block[:, None], row_vals, jnp.zeros_like(row_vals))...  791 us
    gather x1, local copies, waits for them, and re-layouts, device_step(): jnp.take(table_look, jnp.clip(tok_local, 0, vocab_rows - 1), axis=0)  70.5 us
    dot_general x1, matrix products, device_step(): jnp.einsum('td,vd->tv', x_norm, table_head, preferred_element_type=jnp.fl...  69.3 us
  transfers between devices with their start and end apart: 6, of which 2 were waited for; matrix products, arithmetic and copies ran while one was open for 13% of the time, Pallas kernels for 0%

commit v1 on v0

v1 whole, which is shorter than its diff:
```python
import functools
import math
import jax
import numpy as np
import jax.numpy as jnp
from jax import lax
from jax.experimental import pallas as pl
from jax.experimental.pallas import tpu as pltpu
from jax.sharding import PartitionSpec as P

SOFT_CAP = 30.0
NORM_EPS = 1e-6
LOG2E = 1.4426950408889634
TILE = 1024
GROUPS = 1
LOOK_TILE = 2048
GATHER_TILE = 2048
GATHER_GROUP = 128
LANES = 128
CHUNK = 1024
TN_DIMS = (((0,), (0,)), ((), ()))


def spread_ids(ids_ref):
    return jnp.transpose(jnp.broadcast_to(ids_ref[0], (LANES, ids_ref.shape[2])))


def lookup_grad_kernel(scale, row_ref, tok_ref, gx_ref, acc_ref, hit_ref):
    tile = gx_ref.shape[0]
    vocab_rows = acc_ref.shape[1]

    @pl.when(pl.program_id(0) == 0)
    def _():
        acc_ref[...] = jnp.zeros_like(acc_ref)

    tok_off = spread_ids(tok_ref) - row_ref[0] - lax.broadcasted_iota(jnp.int32, (tile, LANES), 1)
    for c in range(0, vocab_rows, LANES):
        hit_ref[:, c:c + LANES] = jnp.where(tok_off == c, scale, 0.0).astype(jnp.bfloat16)
    acc_ref[...] += lax.dot_general(gx_ref[...], hit_ref[...], TN_DIMS, preferred_element_type=jnp.float32)


def head_kernel(total_tokens, tp_ref, h_ref, lab_ref, gain_ref, table_t_ref, table_ref, init_ref,
                dh_ref, acc_ref, dg_ref, loss_ref, *sub_refs):
    tile, width = h_ref.shape
    halves, _, half_rows = table_t_ref.shape
    group = tile // GROUPS
    e_refs, dz_refs, xn_refs = (sub_refs[i * GROUPS:(i + 1) * GROUPS] for i in range(3))
    inv_n = 1.0 / total_tokens

    @pl.when(pl.program_id(0) == 0)
    def _():
        pltpu.sync_copy(init_ref, acc_ref.at[:, :half_rows])
        dg_ref[...] = jnp.zeros_like(dg_ref)
        loss_ref[...] = jnp.zeros_like(loss_ref)

    gain = gain_ref[...]
    lab_off = spread_ids(lab_ref) - lax.broadcasted_iota(jnp.int32, (tile, LANES), 1)
    rows = [slice(g * group, (g + 1) * group) for g in range(GROUPS)]
    inv_rms, sums, labs, lab_w, inv_sum, d_xnorm = ([None] * GROUPS for _ in range(6))

    def norm(g):
        h_wide = h_ref[rows[g], :].astype(jnp.float32)
        inv_rms[g] = lax.rsqrt(jnp.mean(h_wide * h_wide, axis=1, keepdims=True) + NORM_EPS)
        xn_refs[g][...] = (h_wide * inv_rms[g] * gain).astype(jnp.bfloat16)
        sums[g] = jnp.zeros((group, LANES), jnp.float32)
        labs[g] = jnp.zeros((group, LANES), jnp.float32)

    def logits(g, half, c):
        z = jnp.dot(xn_refs[g][...], table_t_ref[half, :, c:c + CHUNK], preferred_element_type=jnp.float32)
        for k in range(c, c + CHUNK, LANES):
            u = jnp.tanh(z[:, k - c:k - c + LANES] * (1.0 / SOFT_CAP))
            e = jnp.exp2((SOFT_CAP * LOG2E) * u)
            e_refs[g][half, :, k:k + LANES] = e * (1.0 - u * u)
            sums[g] += e
            labs[g] = jnp.where(lab_off[rows[g]] == half * half_rows + k, u, labs[g])

    def row_sums(g):
        sum_exp = jnp.sum(sums[g], axis=1, keepdims=True)
        lab_u = jnp.sum(labs[g], axis=1, keepdims=True)
        loss_ref[...] += jnp.log(sum_exp) - SOFT_CAP * lab_u
        inv_sum[g] = jnp.broadcast_to(inv_n / sum_exp, (group, LANES))
        lab_w[g] = jnp.broadcast_to((1.0 - lab_u * lab_u) * inv_n, (group, LANES))

    def d_logits(g, half, c):
        for k in range(c, c + CHUNK, LANES):
            hit = jnp.where(lab_off[rows[g]] == half * half_rows + k, lab_w[g], 0.0)
            dz_refs[g][half, :, k:k + LANES] = (e_refs[g][half, :, k:k + LANES] * inv_sum[g] - hit).astype(jnp.bfloat16)

    def d_xn(g, half):
        part = jnp.dot(dz_refs[g][half], table_ref[half], preferred_element_type=jnp.float32)
        d_xnorm[g] = part if half == 0 else d_xnorm[g] + part

    def d_tab(g):
        own = jnp.where(tp_ref[0] == 0, dz_refs[g][0], dz_refs[g][1])
        acc_ref[:, :half_rows] += lax.dot_general(xn_refs[g][...], own, TN_DIMS, preferred_element_type=jnp.float32)

    def d_hid(g):
        h_norm = h_ref[rows[g], :].astype(jnp.float32) * inv_rms[g]
        g_dir = d_xnorm[g] * gain
        mean_gh = jnp.mean(g_dir * h_norm, axis=1, keepdims=True)
        dh_ref[rows[g], :] = (inv_rms[g] * (g_dir - h_norm * mean_gh)).astype(jnp.bfloat16)
        dg_ref[...] += jnp.sum((d_xnorm[g] * h_norm).reshape(group // 8, 8, width), axis=0)

    chunks = [(half, c) for half in range(halves) for c in range(0, half_rows, CHUNK)]
    norm(0)
    for half, c in chunks:
        logits(0, half, c)
    row_sums(0)
    for half in range(halves):
        for c in range(0, half_rows, CHUNK):
            d_logits(0, half, c)
        d_xn(0, half)
    d_tab(0)
    d_hid(0)

    @pl.when(pl.program_id(0) == pl.num_programs(0) - 1)
    def _():
        dg_cols = jnp.transpose(jnp.broadcast_to(jnp.sum(dg_ref[...], axis=0, keepdims=True), (LANES, width)))
        loss_sum = jnp.sum(loss_ref[...], axis=0, keepdims=True)
        first_lane = lax.broadcasted_iota(jnp.int32, (width, LANES), 1) == 0
        acc_ref[:, half_rows:] = jnp.where(first_lane, dg_cols, loss_sum)


def lookup_kernel(tok_ref, table_ref, out_ref, rows_ref):
    tile = out_ref.shape[0]

    def group_step(g, _):
        base = pl.multiple_of(g * GATHER_GROUP, GATHER_GROUP)
        for t in range(GATHER_GROUP):
            rows_ref[t:t + 1, :] = table_ref[pl.ds(tok_ref[0, 0, base + t], 1), :]
        out_ref[pl.ds(base, GATHER_GROUP), :] = rows_ref[...].astype(jnp.bfloat16)
        return 0

    lax.fori_loop(0, tile // GATHER_GROUP, group_step, 0)


def solution(mesh):
    fsdp_size = mesh.shape["fsdp"]
    tp_size = mesh.shape["tp"]

    def device_step(emb_shard, tok_ids, lab_ids, h_last, g_embed, norm_w):
        vocab_rows, _ = emb_shard.shape
        batch_loc, seq_len, width = h_last.shape
        tok_count = batch_loc * seq_len
        total_tokens = tok_count * fsdp_size
        tp_index = lax.axis_index("tp")
        emb_scale = float(np.asarray(math.sqrt(width), jnp.bfloat16))
        h_rows = h_last.reshape(tok_count, width)
        gx_rows = g_embed.reshape(tok_count, width)
        tok_flat = tok_ids.reshape(tok_count)
        tok_rows = tok_ids.reshape(tok_count // LOOK_TILE, 1, LOOK_TILE)
        lab_rows = lab_ids.reshape(tok_count // TILE, 1, TILE)
        mm_flops = 2 * tok_count * width * vocab_rows

        shard_t = emb_shard.astype(jnp.bfloat16).T
        table_t = lax.all_gather(shard_t, ("tp", "fsdp"), axis=0, tiled=True).reshape(tp_size, width, vocab_rows)
        table = jnp.swapaxes(table_t, 1, 2)
        gain = (1.0 + lax.all_gather(norm_w, "fsdp", axis=0, tiled=True)).reshape(1, width)

        look_t = pl.pallas_call(
            functools.partial(lookup_grad_kernel, emb_scale),
            grid=(tok_count // LOOK_TILE,),
            in_specs=[
                pl.BlockSpec(memory_space=pltpu.SMEM),
                pl.BlockSpec((1, 1, LOOK_TILE), lambda i: (i, 0, 0)),
                pl.BlockSpec((LOOK_TILE, width), lambda i: (i, 0)),
            ],
            out_specs=pl.BlockSpec((width, vocab_rows), lambda i: (0, 0)),
            out_shape=jax.ShapeDtypeStruct((width, vocab_rows), jnp.float32),
            scratch_shapes=[pltpu.VMEM((LOOK_TILE, vocab_rows), jnp.bfloat16)],
            compiler_params=pltpu.CompilerParams(dimension_semantics=("arbitrary",), vmem_limit_bytes=60 * 2**20),
            cost_estimate=pl.CostEstimate(flops=mm_flops, bytes_accessed=tok_count * width * 2, transcendentals=0),
            name="lookup_grad",
        )((tp_index * vocab_rows).reshape(1).astype(jnp.int32), tok_rows, gx_rows)

        once = pl.Buffered(1)
        d_hidden, sums_t = pl.pallas_call(
            functools.partial(head_kernel, total_tokens),
            grid=(tok_count // TILE,),
            in_specs=[
                pl.BlockSpec(memory_space=pltpu.SMEM),
                pl.BlockSpec((TILE, width), lambda i: (i, 0)),
                pl.BlockSpec((1, 1, TILE), lambda i: (i, 0, 0)),
                pl.BlockSpec((1, width), lambda i: (0, 0)),
                pl.BlockSpec((tp_size, width, vocab_rows), lambda i: (0, 0, 0), pipeline_mode=once),
                pl.BlockSpec((tp_size, vocab_rows, width), lambda i: (0, 0, 0), pipeline_mode=once),
                pl.BlockSpec(memory_space=pl.ANY),
            ],
            out_specs=[
                pl.BlockSpec((TILE, width), lambda i: (i, 0)),
                pl.BlockSpec((width, vocab_rows + LANES), lambda i: (0, 0), pipeline_mode=once),
            ],
            out_shape=[
                jax.ShapeDtypeStruct((tok_count, width), jnp.bfloat16),
                jax.ShapeDtypeStruct((width, vocab_rows + LANES), jnp.float32),
            ],
            scratch_shapes=[
                pltpu.VMEM((8, width), jnp.float32),
                pltpu.VMEM((TILE // GROUPS, 1), jnp.float32),
                *[pltpu.VMEM((tp_size, TILE // GROUPS, vocab_rows), jnp.float32)] * GROUPS,
                *[pltpu.VMEM((tp_size, TILE // GROUPS, vocab_rows), jnp.bfloat16)] * GROUPS,
                *[pltpu.VMEM((TILE // GROUPS, width), jnp.bfloat16)] * GROUPS,
            ],
            compiler_params=pltpu.CompilerParams(dimension_semantics=("arbitrary",), vmem_limit_bytes=63 * 2**20),
            cost_estimate=pl.CostEstimate(flops=5 * mm_flops, bytes_accessed=tok_count * width * 4, transcendentals=0),
            name="head",
        )(tp_index.reshape(1).astype(jnp.int32), h_rows, lab_rows, gain, table_t, table, look_t)

        sums = lax.psum_scatter(sums_t, "fsdp", scatter_dimension=0, tiled=True)
        d_table = sums[:, :vocab_rows].T
        d_norm_w = sums[:, vocab_rows]
        loss_val = sums[0, vocab_rows + 1] / total_tokens

        scaled = (table.reshape(tp_size * vocab_rows, width).astype(jnp.float32) * emb_scale).astype(jnp.bfloat16).astype(jnp.float32)
        tok_late, _ = lax.optimization_barrier((tok_flat, sums_t[0, 0]))
        x_emb = pl.pallas_call(
            lookup_kernel,
            grid=(tok_count // GATHER_TILE,),
            in_specs=[
                pl.BlockSpec((1, 1, GATHER_TILE), lambda i: (i, 0, 0), memory_space=pltpu.SMEM),
                pl.BlockSpec((tp_size * vocab_rows, width), lambda i: (0, 0), pipeline_mode=once),
            ],
            out_specs=pl.BlockSpec((GATHER_TILE, width), lambda i: (i, 0)),
            out_shape=jax.ShapeDtypeStruct((tok_count, width), jnp.bfloat16),
            scratch_shapes=[pltpu.VMEM((GATHER_GROUP, width), jnp.float32)],
            compiler_params=pltpu.CompilerParams(dimension_semantics=("arbitrary",), vmem_limit_bytes=48 * 2**20),
            cost_estimate=pl.CostEstimate(flops=2 * mm_flops, bytes_accessed=tok_count * width * 2, transcendentals=0),
            name="lookup",
        )(tok_late.reshape(tok_count // GATHER_TILE, 1, GATHER_TILE), scaled)
        return (x_emb.reshape(batch_loc, seq_len, width), loss_val, d_hidden.reshape(batch_loc, seq_len, width), d_norm_w, d_table)

    spec_tok = P("fsdp", None)
    spec_act = P("fsdp", None, None)
    return jax.shard_map(device_step, mesh=mesh, in_specs=(P("tp", "fsdp"), spec_tok, spec_tok, spec_act, spec_act, P("fsdp")), out_specs=(spec_act, P(), spec_act, P("fsdp"), P("tp", "fsdp")), check_vma=False)
```

time: 2990 us -> 457 us (0.15)
  waiting for transfers between devices: 2400 us -> 0.04 us
  Pallas kernels: 0 us -> 392 us
  other arithmetic: 239 us -> 13.7 us
  matrix products: 215 us -> 0 us
  local copies, waits for them, and re-layouts: 79 us -> 18.1 us
    psum x3 -> x0, waiting for transfers between devices: 2400 us -> none  [the longest x1 1610 us: device_step(): lax.psum(jnp.dot(d_logits, table_head, preferred_element_type=jnp.float32...]
    pallas_call x0 -> x3, Pallas kernels: none -> 392 us  [the longest x1 290 us: device_step(): pl.pallas_call(functools.partial(head_kernel, total_tokens), grid=(tok_co...]
    dot_general x4 -> x0, matrix products: 215 us -> none  [the longest x1 69.3 us: device_step(): jnp.einsum('td,vd->tv', x_norm, table_head, preferred_element_type=jnp.fl...]
    convert_element_type x5 -> x2, other arithmetic: 139 us -> 11.9 us  [device_step(): (table.reshape(tp_size * vocab_rows, width).astype(jnp.float32) * emb_sca...]
    gather x1 -> x0, local copies, waits for them, and re-layouts: 70.5 us -> none  [device_step(): jnp.take(table_look, jnp.clip(tok_local, 0, vocab_rows - 1), axis=0)]
    reduce_sum x3 -> x0, other arithmetic: 58.1 us -> none  [the longest x1 34.8 us: device_step(): jnp.sum(d_xnorm * h_norm, axis=0)]
  transfers between devices with their start and end apart: 6 -> 2, of which waited for: 2 -> 0; matrix products, arithmetic and copies ran while one was open for 13% -> 3% of each run, Pallas kernels for 0% -> 22%
where the time goes in v1:
time: 457 us; the launch traced here: 456 us
  Pallas kernels  392 us (86%)
  local copies, waits for them, and re-layouts  18.1 us (4%)
  between operations  16.5 us (4%)
  blocking collectives  15.9 us (3%)
  other arithmetic  13.7 us (3%)
    pallas_call x1, Pallas kernels, device_step(): pl.pallas_call(functools.partial(head_kernel, total_tokens), grid=(tok_co...  290 us
    pallas_call x1, Pallas kernels, device_step(): pl.pallas_call(lookup_kernel, grid=(tok_count // GATHER_TILE,), in_specs=...  53.2 us
    pallas_call x1, Pallas kernels, device_step(): pl.pallas_call(functools.partial(lookup_grad_kernel, emb_scale), grid=(to...  48.3 us
    unnamed x1, blocking collectives  15.9 us
    convert_element_type x2, other arithmetic, device_step(): (table.reshape(tp_size * vocab_rows, width).astype(jnp.float32) * emb_sca...  11.9 us
  transfers between devices with their start and end apart: 2, of which 0 were waited for; matrix products, arithmetic and copies ran while one was open for 3% of the time, Pallas kernels for 22%

profile of v1, /device:TPU:0, one launch (start us, length us, event | category | flops | bytes accessed | tf_op | source)
XLA Modules:
  0.0 456.1 jit_solution(13319112855252668642)
XLA Ops:
  7.2 0.0 all-gather.2.cloned.1.call-start
  7.2 1.8 convert_bitcast_fusion
  9.0 0.0 all-gather.2.cloned.1.call-update
  9.1 0.0 reduce-scatter.2.cloned.1.call-start
  9.1 1.6 reshape.64.tok_ref
  10.7 1.2 dynamic-slice
  12.6 0.9 dynamic-update-slice
  13.5 15.9 %all-reduce = f32[1152]{0:T(1024)S(1)} all-reduce(f32[1152]{0:T(1024)S(1)} %dynamic-update-slice), channel_id=1, replica_groups=mesh['tp'=2,'fsdp'=8] {'fsdp'}, use_global_device_ids=true, to_apply=%add | all-reduce | flops 1152 | bytes 9216
  29.4 0.6 reshape.62.gain_ref
  30.0 1.6 reshape.61.lab_ref
  31.5 0.8 copy.13
  32.4 48.3 %lookup_grad.1.init_ref = f32[1152,1024]{1,0:T(8,128)} custom-call(s32[1]{0:T(128)} %bitcast.9.row_ref, s32[8,1,2048]{2,1,0:T(1,128)} %reshape.64.tok_ref, bf16[16384,1152]{1,0:T(8,128)(2,1)} %bitcast.26), custom_call_target="tpu_custom_call" | custom-call | flops 38654705664 | bytes 37748736 | tf_op jit(solution)/shard_map/lookup_grad/pallas_call | solution.py:160
  80.6 0.0 all-gather.2.cloned.1.call-done
  80.6 6.6 %copy.12 = bf16[2,1152,1024]{1,2,0:T(8,128)(2,1)} copy(bf16[2,1152,1024]{2,1,0:T(8,128)(2,1)} %bitcast.23) | data formatting | bytes 9437184 | tf_op jit(solution)/shard_map/reshape | solution.py:156
  87.3 5.3 %multiply_convert_fusion = bf16[2,1024,1152]{2,1,0:T(8,128)(2,1)} fusion(bf16[2,1152,1024]{1,2,0:T(8,128)(2,1)} %copy.12), kind=kLoop, calls=%fused_computation | loop fusion | flops 7077888 | bytes 9437184 | tf_op jit(solution)/shard_map/convert_element_type | solution.py:214
  92.6 290.3 %head.1 = (bf16[16384,1152]{1,0:T(8,128)(2,1)}, f32[1152,1152]{1,0:T(8,128)}) custom-call(s32[1]{0:T(128)} %bitcast.6.tp_ref, bf16[16384,1152]{1,0:T(8,128)(2,1)} %bitcast.27, s32[16,1,1024]{2,1,0:T(1,128)} %reshape.61.lab_ref, f32[1,1152]{1,0:T(1,128)} %reshape.62.gain_ref, bf16[2,1152,1024]{2,1,0:T(8,128)(2,1)} %bitcast.24, ...), custom_call_target="tpu_custom_call" | custom-call | flops 193273528320 | bytes 75497472 | tf_op jit(solution)/shard_map/head/pallas_call | solution.py:177
  382.9 0.0 reduce-scatter.2.cloned.1.call-update
  383.0 6.6 %bitcast_convert_fusion.table_ref = f32[2048,1152]{1,0:T(8,128)} fusion(bf16[2,1024,1152]{2,1,0:T(8,128)(2,1)} %multiply_convert_fusion), kind=kLoop, calls=%fused_computation.1 | loop fusion | flops 2359296 | bytes 14155776 | tf_op jit(solution)/shard_map/convert_element_type | solution.py:214
  389.5 53.2 %lookup.1 = bf16[16384,1152]{1,0:T(8,128)(2,1)} custom-call(s32[8,1,2048]{2,1,0:T(1,128)S(1)} %bitcast.21, f32[2048,1152]{1,0:T(8,128)} %bitcast_convert_fusion.table_ref), custom_call_target="tpu_custom_call" | custom-call | flops 77309411328 | bytes 37748736 | tf_op jit(solution)/shard_map/lookup/pallas_call | solution.py:216
  442.7 0.0 reduce-scatter.2.cloned.1.call-done
  442.7 1.3 slice.13
  444.6 1.9 slice_bitcast_fusion
  446.6 1.6 slice_reduce_fusion
  (2 shorter events, 0.0 us)
Async XLA Ops:
  7.2 73.5 %all-gather.2.cloned.1.call-start = ((), (), s32[]{:S(2)}) async-start(), calls=%async_computation.1 | async-start | bytes 5013504 | tf_op jit(solution)/shard_map/all_gather | solution.py:156
  9.1 433.7 %reduce-scatter.2.cloned.1.call-start = ((), (), s32[]{:S(2)}) async-start(), calls=%async_computation.2 | async-start | bytes 5971968 | tf_op jit(solution)/shard_map/reduce_scatter | solution.py:209
Sparse Core Ops, SparseCore 0:
  10.8 39.5 all-gather.1
  383.1 49.9 reduce-scatter.1
